TPU v7x, 32 devices: a whole 2x2x4 slice. The times are simulated.
32 devices in a mesh: row: 8 (over y, x, core), col: 4 (over z).
Axes of the slice: x: 2, y: 2, z: 4, core: 2. Of those that a mesh axis runs over, the one named last changes fastest.
Arguments:
- queries: bfloat16 [8, 128, 4096], P(None, 'row', 'col'), may hold values from -13 to 13, as said below
- key_cache: bfloat16 [8, 16384, 1024], P(None, ('row', 'col')), may hold values from -13 to 13
- value_cache: bfloat16 [8, 16384, 1024], P(None, ('row', 'col')), may hold values from -6 to 6
- key_table: bfloat16 [1024, 1024], replicated, may hold values from -24 to 24
- value_table: bfloat16 [1024, 1024], replicated, may hold values from -6 to 6
- lengths: int32 [8], replicated, may hold values from 2048 to 16384
- token_ids: int32 [8, 128], P(None, 'row'), may hold values from 0 to 1023
Outputs:
- attended: bfloat16 [8, 128, 4096], P(None, 'row', 'col')
Inputs may be any that keep to these rules, and one draw needn't show every extreme that they name: `queries`: entries of the query array lie in the stated range.
All inputs are finite; a program needn't handle non-finite values.
Results may differ from a plain program's by a relative error of at most 0.006.
Values may be sent and summed in bfloat16 or wider, within the bound.
A program may use at most 192 MiB of HBM per device.

v0:
```python
import jax
import jax.numpy as jnp
from jax import lax
from jax.sharding import PartitionSpec as P

HQ = 32
KH = 8
HD = 128


def cache_partials(whole, key_cache, value_cache, lengths, offset):
    users, beams, width = whole.shape
    positions = key_cache.shape[1]
    group = HQ // KH
    scale = HD ** (-0.5)

    def one_user(items):
        q_user, k_user, v_user, limit = items
        q_heads = q_user.reshape(beams, KH, group, HD)
        k_heads = k_user.reshape(positions, KH, HD)
        v_heads = v_user.reshape(positions, KH, HD)
        s = (
            jnp.einsum("wkgd,lkd->kwgl", q_heads, k_heads, preferred_element_type=jnp.float32)
            * scale
        )
        live = offset + jnp.arange(positions, dtype=jnp.int32) < limit
        s = jnp.where(live, s, -1e30)
        peak = jnp.max(s, axis=-1)
        weight = jnp.where(live, jnp.exp(s - peak[..., None]), 0.0)
        total = jnp.sum(weight, axis=-1)
        numer = jnp.einsum(
            "kwgl,lkd->wkgd",
            weight.astype(jnp.bfloat16),
            v_heads,
            preferred_element_type=jnp.float32,
        )
        peak = jnp.transpose(peak, (1, 0, 2)).reshape(beams, HQ)
        total = jnp.transpose(total, (1, 0, 2)).reshape(beams, HQ)
        return (numer.reshape(beams, width), peak, total)

    return lax.map(one_user, (whole, key_cache, value_cache, lengths))


def body(queries, key_cache, value_cache, key_table, value_table, lengths, token_ids):
    users, beam_part, width_part = queries.shape
    heads_part = width_part // HD
    scale = HD ** (-0.5)
    row_at = lax.axis_index("row")
    col_at = lax.axis_index("col")
    whole = lax.all_gather(queries, "col", axis=2, tiled=True)
    whole = lax.all_gather(whole, "row", axis=1, tiled=True)
    offset = (row_at * lax.axis_size("col") + col_at) * key_cache.shape[1]
    numer_part, peak_part, total_part = cache_partials(
        whole, key_cache, value_cache, lengths, offset
    )
    peak_all = lax.pmax(peak_part, ("row", "col"))
    factor = jnp.exp(peak_part - peak_all)
    weighted = (numer_part.reshape(users, -1, HQ, HD) * factor[..., None]).reshape(
        users, -1, HQ * HD
    )
    mass = total_part * factor

    def local_part(array, per_head):
        picked = lax.dynamic_slice_in_dim(array, row_at * beam_part, beam_part, 1)
        return lax.dynamic_slice_in_dim(
            picked, col_at * heads_part * per_head, heads_part * per_head, 2
        )

    numer, total = lax.psum((weighted, mass), ("row", "col"))
    numer = local_part(numer, HD)
    total = local_part(total, 1)
    peak = local_part(peak_all, 1)
    codes = jnp.arange(key_table.shape[0], dtype=jnp.int32)
    onehot = (token_ids[..., None] == codes).astype(jnp.bfloat16)
    own_keys = jnp.einsum("uwv,vc->uwc", onehot, key_table, preferred_element_type=jnp.float32)
    own_values = jnp.einsum("uwv,vc->uwc", onehot, value_table, preferred_element_type=jnp.float32)
    group = HQ // KH
    own_keys = jnp.repeat(own_keys.reshape(users, beam_part, KH, HD), group, axis=2)
    own_values = jnp.repeat(own_values.reshape(users, beam_part, KH, HD), group, axis=2)
    own_keys = lax.dynamic_slice_in_dim(own_keys, col_at * heads_part, heads_part, 2)
    own_values = lax.dynamic_slice_in_dim(own_values, col_at * heads_part, heads_part, 2)
    q_local = queries.astype(jnp.float32).reshape(users, beam_part, heads_part, HD)
    own_score = jnp.sum(q_local * own_keys, axis=-1) * scale
    final_peak = jnp.maximum(peak, own_score)
    carried = jnp.exp(peak - final_peak)
    fresh = jnp.exp(own_score - final_peak)
    numer = (
        numer.reshape(users, beam_part, heads_part, HD) * carried[..., None]
        + fresh[..., None] * own_values
    )
    total = total * carried + fresh
    result = numer / total[..., None]
    return result.reshape(users, beam_part, width_part).astype(jnp.bfloat16)


def solution(mesh):
    return jax.shard_map(
        body,
        mesh=mesh,
        in_specs=(
            P(None, "row", "col"),
            P(None, ("row", "col"), None),
            P(None, ("row", "col"), None),
            P(),
            P(),
            P(),
            P(None, "row"),
        ),
        out_specs=P(None, "row", "col"),
        check_vma=False,
    )
```

profile of v0, /device:TPU:0, one launch (start us, length us, event | category | flops | bytes accessed | tf_op | source)
XLA Modules:
  0.0 730.9 jit_solution(4568035272929321944)
XLA Ops:
  8.6 31.1 %all-gather.3.cloned.1.call-done = bf16[8,16,4096]{2,0,1:T(8,128)(2,1)} async-done(((bf16[8,16,1024]{2,0,1:T(8,128)(2,1)}), bf16[8,16,4096]{2,0,1:T(8,128)(2,1)}) %all-gather.3.cloned.1.call-update) | async-done | bytes 1048592 | tf_op jit(solution)/shard_map/all_gather | solution.py:50
  39.8 55.4 %all-gather.5.cloned.1.call-done = bf16[8,128,4096]{2,0,1:T(8,128)(2,1)} async-done(((bf16[8,16,4096]{2,0,1:T(8,128)(2,1)}), bf16[8,128,4096]{2,0,1:T(8,128)(2,1)}) %all-gather.5.cloned.1.call-update) | async-done | bytes 8388624 | tf_op jit(solution)/shard_map/all_gather | solution.py:51
  95.2 12.5 %copy.37 = bf16[8,128,4096]{1,2,0:T(8,128)(2,1)} copy(bf16[8,128,4096]{2,0,1:T(8,128)(2,1)} %all-gather.5.cloned.1.call-done) | data formatting | bytes 16777216 | tf_op jit(solution)/shard_map/while | solution.py:41
  107.7 186.9 %while.14 = (s32[]{:T(128)}, f32[8,128,4096]{1,2,0:T(8,128)}, f32[8,128,32]{1,2,0:T(8,128)}, f32[8,128,32]{1,2,0:T(8,128)S(1)}, bf16[8,512,1024]{2,1,0:T(8,128)(...) while((s32[]{:T(128)}, f32[8,128,4096]{1,2,0:T(8,128)}, ...), condition=%wide.region_3.4_spmd, body=%wide.region_0.3_spmd.sunk | while | flops 1100997632 | bytes 78777504 | solution.py:41
  115.8 3.2 copy-done.1
  124.6 5.0 fusion.36
  139.1 3.2 copy-done.1
  148.0 5.0 fusion.36
  162.5 3.2 copy-done.1
  171.3 5.0 fusion.36
  185.8 3.2 copy-done.1
  194.7 5.0 fusion.36
  209.2 3.2 copy-done.1
  218.1 5.0 fusion.36
  232.6 3.2 copy-done.1
  241.4 5.0 fusion.36
  256.0 3.2 copy-done.1
  264.8 5.0 fusion.36
  279.3 3.2 copy-done.1
  288.2 5.0 fusion.36
  294.7 124.8 %all-reduce.4.cloned.1.call-done = f32[8,128,32]{1,2,0:T(8,128)} async-done(((f32[8,128,32]{1,2,0:T(8,128)}), f32[8,128,32]{1,2,0:T(8,128)}) %all-reduce.4.cloned.1.call-update) | async-done | bytes 131088 | tf_op jit(solution)/shard_map/pmax | solution.py:56
  421.1 11.3 %bitcast_multiply_fusion = f32[8,128,4096]{1,2,0:T(8,128)} fusion(f32[8,128,4096]{1,2,0:T(8,128)} %get-tuple-element.54, f32[8,128,32]{1,2,0:T(8,128)S(1)} %get-tuple-element.117), kind=kLoop, calls=%fused_computation.17 | loop fusion | flops 4194304 | bytes 33685504 | tf_op jit(solution)/shard_map/mul | solution.py:58
  436.8 276.3 %all-reduce.6.cloned.1.call-done = (f32[8,128,4096]{1,2,0:T(8,128)}, f32[8,128,32]{1,2,0:T(8,128)}) async-done(((f32[8,128,4096]{1,2,0:T(8,128)}, f32[8,128,32]{1,2,0:T(8,128)}), (f32[8,128,4096]{1,2,0:T(8,128)}, f32[8,128,32]{1,2,0:T(8,128)})) %all-reduce.6.cloned.1.call-update) | async-done | bytes 16908304 | tf_op jit(solution)/shard_map/psum | solution.py:69
  714.4 5.3 constant_dynamic-slice_fusion.3
  (133 shorter events, 135.2 us)
Async XLA Ops:
  6.5 425.9 %copy-start = (bf16[1024,1024]{1,0:T(8,128)(2,1)S(1)}, bf16[1024,1024]{1,0:T(8,128)(2,1)}, u32[]{:S(2)}) copy-start(bf16[1024,1024]{1,0:T(8,128)(2,1)} %param.12) | copy-start | bytes 6291460
  6.5 33.1 %all-gather.3.cloned.1.call-start = ((), (), s32[]{:S(2)}) async-start(), calls=%async_computation | async-start | bytes 1310720 | tf_op jit(solution)/shard_map/all_gather | solution.py:50
  8.5 86.7 %all-gather.5.cloned.1.call-start = ((), (), s32[]{:S(2)}) async-start(), calls=%async_computation.1 | async-start | bytes 9437184 | tf_op jit(solution)/shard_map/all_gather | solution.py:51
  39.7 379.7 %all-reduce.4.cloned.1.call-start = ((), (), s32[]{:S(2)}) async-start(), calls=%async_computation.2 | async-start | bytes 262144 | tf_op jit(solution)/shard_map/pmax | solution.py:56
  39.8 67.9 %copy-start.4 = (s32[8]{0:T(128)S(1)}, s32[8]{0:T(128)}, u32[]{:S(2)}) copy-start(s32[8]{0:T(128)} %param.14) | copy-start | bytes 100
  115.8 3.2 copy-start.1
  139.1 3.2 copy-start.1
  162.5 3.2 copy-start.1
  185.8 3.2 copy-start.1
  209.2 3.2 copy-start.1
  232.6 3.2 copy-start.1
  256.0 3.2 copy-start.1
  279.3 3.2 copy-start.1
  294.6 418.6 %all-reduce.6.cloned.1.call-start = ((), (), s32[]{:S(2)}) async-start(), calls=%async_computation.3 | async-start | bytes 33816576 | tf_op jit(solution)/shard_map/psum | solution.py:69
  432.4 0.7 copy-start.3
  432.4 1.3 copy-start.2
Sparse Core Ops, SparseCore 0:
  8.9 30.6 all-gather.2
  41.5 53.6 all-gather.4
  294.7 124.6 all-reduce.3
  432.5 280.6 all-reduce.5
where the time goes:
time: 733 us; the launch traced here: 731 us
  waiting for transfers between devices  488 us (67%)
  local copies, waits for them, and re-layouts  126 us (17%)
  matrix products  65 us (9%)
  other arithmetic  38.3 us (5%)
  between operations  13.3 us (2%)
    psum x1, waiting for transfers between devices, body(): numer, total = lax.psum((weighted, mass), ('row', 'col'))  276 us
    pmax x1, waiting for transfers between devices, body(): peak_all = lax.pmax(peak_part, ('row', 'col'))  125 us
    dynamic_slice x48, local copies, waits for them, and re-layouts, cache_partials(): return lax.map(one_user, (whole, key_cache, value_cache, lengths))  58 us
    all_gather x1, waiting for transfers between devices, body(): whole = lax.all_gather(whole, 'row', axis=1, tiled=True)  55.4 us
    dot_general x8, matrix products, one_user(): jnp.einsum('kwgl,lkd->wkgd', weight.astype(jnp.bfloat16), v_heads, prefer...  39.7 us
    all_gather x1, waiting for transfers between devices, body(): whole = lax.all_gather(queries, 'col', axis=2, tiled=True)  31.1 us
    while x16, local copies, waits for them, and re-layouts  25.8 us
    dot_general x8, matrix products, one_user(): jnp.einsum('wkgd,lkd->kwgl', q_heads, k_heads, preferred_element_type=jnp...  22.7 us
  transfers between devices with their start and end apart: 4, of which 4 were waited for; matrix products, arithmetic and copies ran while one was open for 1% of the time, Pallas kernels for 0%

commit v1 on v0

v1 whole, which is shorter than its diff:
```python
import functools
import math

import jax
import jax.numpy as jnp
from jax import lax
from jax.experimental import pallas as pl
from jax.experimental.pallas import tpu as pltpu
from jax.sharding import PartitionSpec as P

HQ = 32
KH = 8
HD = 128
GROUP = HQ // KH
CHUNKS = 2
LOG2E = math.log2(math.e)
MESH = pl.DeviceIdType.MESH


def attend_kernel(live_ref, q_ref, k_ref, v_ref, o_ref, m_ref, l_ref):
    rows, cols, _, piece, _ = q_ref.shape
    positions = k_ref.shape[1]
    kv_part = KH // cols
    part = piece // kv_part
    factor = HD ** (-0.5) * LOG2E
    live = live_ref[pl.program_id(0)]

    def run(masked):
        if masked:
            keep = lax.broadcasted_iota(jnp.int32, (positions, rows * part), 0) < live
        for j in range(KH):
            c, at = divmod(j, kv_part)
            span = slice(at * part, (at + 1) * part)
            q = q_ref[:, c, 0, span, :].reshape(rows * part, HD)
            k = k_ref[0, :, j * HD : (j + 1) * HD]
            s = lax.dot_general(k, q, (((1,), (1,)), ((), ())), preferred_element_type=jnp.float32)
            if masked:
                s = jnp.where(keep, s, -1e30)
            m = jnp.max(s, axis=0, keepdims=True)
            p = jnp.exp2((s - m) * factor)
            l_ref[0, j : j + 1, :] = jnp.sum(p, axis=0, keepdims=True)
            m_ref[0, j : j + 1, :] = m * factor
            v = v_ref[0, :, j * HD : (j + 1) * HD]
            o = lax.dot_general(
                v, p.astype(jnp.bfloat16), (((0,), (0,)), ((), ())), preferred_element_type=jnp.float32
            )
            o_ref[:, c, 0, span, :] = o.T.astype(jnp.bfloat16).reshape(rows, part, HD)

    @pl.when(live >= positions)
    def _():
        run(False)

    @pl.when((live > 0) & (live < positions))
    def _():
        run(True)

    @pl.when(live <= 0)
    def _():
        o_ref[...] = jnp.zeros_like(o_ref)
        m_ref[...] = jnp.full_like(m_ref, -1e30)
        l_ref[...] = jnp.zeros_like(l_ref)


def attend(live, gathered, keys, values, first):
    rows, cols, users, piece, _ = gathered.shape
    _, positions, width = keys.shape
    stat = rows * piece * cols // KH
    q_spec = pl.BlockSpec((rows, cols, 1, piece, HD), lambda u, live: (0, 0, u, 0, 0))
    c_spec = pl.BlockSpec((1, positions, width), lambda u, live: (u + first, 0, 0))
    s_spec = pl.BlockSpec((1, KH, stat), lambda u, live: (u, 0, 0))
    scores = users * KH * stat * positions
    return pl.pallas_call(
        attend_kernel,
        grid_spec=pltpu.PrefetchScalarGridSpec(
            num_scalar_prefetch=1,
            grid=(users,),
            in_specs=[q_spec, c_spec, c_spec],
            out_specs=[q_spec, s_spec, s_spec],
        ),
        out_shape=[
            jax.ShapeDtypeStruct(gathered.shape, jnp.bfloat16),
            jax.ShapeDtypeStruct((users, KH, stat), jnp.float32),
            jax.ShapeDtypeStruct((users, KH, stat), jnp.float32),
        ],
        compiler_params=pltpu.CompilerParams(
            dimension_semantics=("arbitrary",), vmem_limit_bytes=40 * 1024 * 1024
        ),
        cost_estimate=pl.CostEstimate(
            flops=4 * scores * HD * 2,
            bytes_accessed=4 * gathered.size + 4 * users * positions * width,
            transcendentals=scores,
        ),
        name="attend",
    )(live, gathered, keys, values)


def merge(pieces, n):
    peak = functools.reduce(jnp.maximum, [x[:n] for x in pieces])
    total = sum(x[n:] * jnp.exp2(x[:n] - peak) for x in pieces)
    return peak, total


def peaks_kernel(
    st_ref, all_ref, own_ref, row_in, col_out, col_in, row_all, send_sem, recv_sem
):
    rows, cols, two, _ = st_ref.shape
    n = two // 2
    me = {"row": lax.axis_index("row"), "col": lax.axis_index("col")}
    size = {"row": rows, "col": cols}

    def peer(axis, step):
        return {axis: lax.rem(me[axis] + step, size[axis])}

    others = [(axis, step) for axis in ("row", "col") for step in range(1, size[axis])]
    barrier = pltpu.get_barrier_semaphore()
    for axis, step in others:
        pl.semaphore_signal(barrier, inc=1, device_id=peer(axis, step), device_id_type=MESH)
    pl.semaphore_wait(barrier, len(others))

    taken = [0]

    def exchange(axis, source, target):
        copies = []
        for step in range(1, size[axis]):
            to = peer(axis, step)
            copy = pltpu.make_async_remote_copy(
                src_ref=source(to[axis]),
                dst_ref=target(step),
                send_sem=send_sem.at[taken[0]],
                recv_sem=recv_sem.at[taken[0]],
                device_id=to,
                device_id_type=MESH,
            )
            taken[0] += 1
            copy.start()
            copies.append(copy)
        for copy in copies:
            copy.wait()

    exchange("row", lambda to: st_ref.at[to], lambda step: row_in.at[step - 1])
    mine = st_ref[me["row"]]
    for c in range(cols):
        peak, total = merge([mine[c]] + [row_in[step, c] for step in range(rows - 1)], n)
        col_out[c, :n] = peak
        col_out[c, n:] = total
    exchange("col", lambda to: col_out.at[to], lambda step: col_in.at[step - 1])
    peak, total = merge([col_out[me["col"]]] + [col_in[step] for step in range(cols - 1)], n)
    own_ref[:n] = peak
    own_ref[n:] = total
    here = row_all.at[me["row"]]
    here[me["col"]] = peak
    spot = here.at[me["col"]]
    exchange("col", lambda to: spot, lambda step: spot)
    exchange("row", lambda to: here, lambda step: here)
    all_ref[...] = row_all[...]


def peaks(stats):
    rows, cols, two, lanes = stats.shape
    n = two // 2
    sends = 2 * (rows - 1) + 2 * (cols - 1)
    vmem = pl.BlockSpec(memory_space=pltpu.VMEM)
    return pl.pallas_call(
        peaks_kernel,
        out_shape=[
            jax.ShapeDtypeStruct((rows, cols, n, lanes), jnp.float32),
            jax.ShapeDtypeStruct((two, lanes), jnp.float32),
        ],
        in_specs=[vmem],
        out_specs=[vmem, vmem],
        scratch_shapes=[
            pltpu.VMEM((rows - 1, cols, two, lanes), jnp.float32),
            pltpu.VMEM((cols, two, lanes), jnp.float32),
            pltpu.VMEM((cols - 1, two, lanes), jnp.float32),
            pltpu.VMEM((rows, cols, n, lanes), jnp.float32),
            pltpu.SemaphoreType.DMA((sends,)),
            pltpu.SemaphoreType.DMA((sends,)),
        ],
        compiler_params=pltpu.CompilerParams(collective_id=0, has_side_effects=True),
        name="peaks",
    )(stats)


def body(queries, key_cache, value_cache, key_table, value_table, lengths, token_ids):
    users, beam_part, width_part = queries.shape
    heads_part = width_part // HD
    kv_part = heads_part // GROUP
    rows, cols = lax.axis_size("row"), lax.axis_size("col")
    row_at, col_at = lax.axis_index("row"), lax.axis_index("col")
    positions = key_cache.shape[1]
    offset = (row_at * cols + col_at) * positions
    live = jnp.clip(lengths - offset, 0, positions)
    piece = heads_part * beam_part
    q_local = queries.reshape(users, beam_part, heads_part, HD).transpose(0, 2, 1, 3)
    q_local = q_local.reshape(users, piece, HD)
    some = users // CHUNKS

    gathered = [
        lax.all_gather(q_local[i * some : (i + 1) * some], ("row", "col"), axis=0)
        for i in range(CHUNKS)
    ]

    own_keys, own_values = (
        jnp.einsum(
            "uwv,vc->uwc",
            (token_ids[..., None] == jnp.arange(table.shape[0], dtype=jnp.int32)).astype(jnp.bfloat16),
            lax.dynamic_slice_in_dim(table, col_at * kv_part * HD, kv_part * HD, 1),
            preferred_element_type=jnp.float32,
        )
        .reshape(users, beam_part, kv_part, HD)
        .transpose(0, 2, 1, 3)[:, :, None]
        for table in (key_table, value_table)
    )
    q_heads = q_local.astype(jnp.float32).reshape(users, kv_part, GROUP, beam_part, HD)
    own_score = jnp.sum(q_heads * own_keys, axis=-1) * (HD ** (-0.5) * LOG2E)

    outs = []
    for i in range(CHUNKS):
        span = slice(i * some, (i + 1) * some)
        numer, m, l = attend(
            live[span],
            gathered[i].reshape(rows, cols, some, piece, HD),
            key_cache,
            value_cache,
            i * some,
        )

        def by_device(x):
            x = x.reshape(some, cols, kv_part, rows, piece // kv_part)
            return x.transpose(3, 1, 0, 2, 4).reshape(rows, cols, some * piece // HD, HD)

        m = by_device(m)
        peak_all, own = peaks(jnp.concatenate([m, by_device(l)], axis=2))
        factor = jnp.exp2(m - peak_all).reshape(rows * cols, some, piece)
        weighted = numer.reshape(rows * cols, some, piece, HD).astype(jnp.float32) * factor[..., None]
        numer = lax.psum_scatter(
            weighted.astype(jnp.bfloat16), ("row", "col"), scatter_dimension=0, tiled=False
        )
        numer = numer.astype(jnp.float32).reshape(some, kv_part, GROUP, beam_part, HD)
        peak, total = own.reshape(2, some, kv_part, GROUP, beam_part)
        e = own_score[span]
        top = jnp.maximum(peak, e)
        carried = jnp.exp2(peak - top)
        fresh = jnp.exp2(e - top)
        numer = numer * carried[..., None] + fresh[..., None] * own_values[span]
        outs.append(numer / (total * carried + fresh)[..., None])
    result = jnp.concatenate(outs).reshape(users, heads_part, beam_part, HD)
    return result.transpose(0, 2, 1, 3).reshape(users, beam_part, width_part).astype(jnp.bfloat16)


def solution(mesh):
    return jax.shard_map(
        body,
        mesh=mesh,
        in_specs=(
            P(None, "row", "col"),
            P(None, ("row", "col"), None),
            P(None, ("row", "col"), None),
            P(),
            P(),
            P(),
            P(None, "row"),
        ),
        out_specs=P(None, "row", "col"),
        check_vma=False,
    )
```

time: 733 us -> 449 us (0.61)
  waiting for transfers between devices: 488 us -> 322 us
  local copies, waits for them, and re-layouts: 126 us -> 14.9 us
  Pallas kernels: 0 us -> 78.6 us
  matrix products: 65 us -> 1.61 us
  other arithmetic: 38.3 us -> 18.3 us
    psum x1 -> x0, waiting for transfers between devices: 276 us -> none  [body(): numer, total = lax.psum((weighted, mass), ('row', 'col'))]
    reduce_scatter x0 -> x2, waiting for transfers between devices: none -> 244 us  [body(): lax.psum_scatter(weighted.astype(jnp.bfloat16), ('row', 'col'), scatter_d...]
    pmax x1 -> x0, waiting for transfers between devices: 125 us -> none  [body(): peak_all = lax.pmax(peak_part, ('row', 'col'))]
    pallas_call x0 -> x4, Pallas kernels: none -> 78.6 us  [the longest x2 42 us: attend(): pl.pallas_call(attend_kernel, grid_spec=pltpu.PrefetchScalarGridSpec(num_...]
    dot_general x18 -> x2, matrix products: 65 us -> 1.61 us  [body(): jnp.einsum('uwv,vc->uwc', (token_ids[..., None] == jnp.arange(table.shape...]
    dynamic_slice x49 -> x0, local copies, waits for them, and re-layouts: 63.3 us -> none  [the longest x48 58 us: cache_partials(): return lax.map(one_user, (whole, key_cache, value_cache, lengths))]
    while x17 -> x0, local copies, waits for them, and re-layouts: 38.3 us -> none
    reduce_sum x9 -> x1, other arithmetic: 19 us -> 0.21 us  [body(): own_score = jnp.sum(q_heads * own_keys, axis=-1) * (HD ** (-0.5) * LOG2E)]
  transfers between devices with their start and end apart: 4 -> 4, of which waited for: 4 -> 4; matrix products, arithmetic and copies ran while one was open for 1% -> 5% of each run, Pallas kernels for 0% -> 18%
where the time goes in v1:
time: 449 us
  waiting for transfers between devices  322 us (72%)
  Pallas kernels  78.6 us (18%)
  other arithmetic  18.3 us (4%)
  local copies, waits for them, and re-layouts  14.9 us (3%)
  between operations  13.4 us (3%)
    reduce_scatter x2, waiting for transfers between devices, body(): lax.psum_scatter(weighted.astype(jnp.bfloat16), ('row', 'col'), scatter_d...  244 us
    all_gather x2, waiting for transfers between devices, body(): lax.all_gather(q_local[i * some:(i + 1) * some], ('row', 'col'), axis=0)  77.3 us
    pallas_call x2, Pallas kernels, attend(): pl.pallas_call(attend_kernel, grid_spec=pltpu.PrefetchScalarGridSpec(num_...  42 us
    pallas_call x2, Pallas kernels, peaks(): pl.pallas_call(peaks_kernel, out_shape=[jax.ShapeDtypeStruct((rows, cols,...  36.6 us
    convert_element_type x2, other arithmetic, body(): weighted.astype(jnp.bfloat16)  11.9 us
    unnamed x17, local copies, waits for them, and re-layouts  10.1 us
  transfers between devices with their start and end apart: 4, of which 4 were waited for; matrix products, arithmetic and copies ran while one was open for 5% of the time, Pallas kernels for 18%

profile of v1, /device:TPU:0, one launch (start us, length us, event | category | flops | bytes accessed | tf_op | source)
XLA Modules:
  0.0 448.7 jit_solution(559309765947908233)
XLA Ops:
  6.5 1.1 copy.56
  7.7 0.7 copy.40
  10.0 64.7 %all-gather.3.cloned.1.call-done = bf16[32,4,128,128]{3,2,1,0:T(8,128)(2,1)} async-done(((bf16[1,4,128,128]{3,2,1,0:T(8,128)(2,1)}), bf16[32,4,128,128]{3,2,1,0:T(8,128)(2,1)}) %all-gather.3.cloned.1.call-update) | async-done | bytes 4194320 | tf_op jit(solution)/shard_map/all_gather | solution.py:199
  74.7 2.2 copy-done.4
  76.9 21.0 %attend.2 = (bf16[8,4,4,128,128]{4,3,2,1,0:T(8,128)(2,1)S(1)}, f32[4,8,512]{2,1,0:T(8,128)S(1)}, f32[4,8,512]{2,1,0:T(8,128)S(1)}) custom-call(s32[4]{0:T(128)S(1)} %get-tuple-element.41.live_ref, bf16[8,4,4,128,128]{4,3,2,1,0:T(8,128)(2,1)S(1)} %bitcast.65, bf16[8,512,1024]{2,1,0:T(8,128)(2,1)} %k_ref.3, bf16[8,512,1024]{2,1,0:T(8,128)(2,1)} %v_ref.3), custom_call_target="tpu_custom_call" | custom-call | flops 8589934592 | bytes 16777216 | tf_op jit(solution)/shard_map/attend/pallas_call | solution.py:72
  97.9 2.0 copy-done.1
  100.5 0.7 pad_maximum_fusion.st_ref
  101.2 18.6 %peaks.2 = (f32[8,4,4,128]{3,2,1,0:T(4,128)}, f32[8,128]{1,0:T(8,128)}) custom-call(f32[8,4,8,128]{3,2,1,0:T(8,128)} %pad_maximum_fusion.st_ref), custom_call_target="tpu_custom_call" | custom-call | tf_op jit(solution)/shard_map/peaks/pallas_call | solution.py:163
  119.7 0.9 multiply_exponential_fusion.1
  120.6 6.0 %fusion.1 = bf16[32,4,128,128]{3,2,1,0:T(8,128)(2,1)} fusion(bf16[8,4,4,128,128]{4,3,2,1,0:T(8,128)(2,1)} %copy-done.1, f32[32,4,128]{2,1,0:T(4,128)S(1)} %bitcast.79), kind=kLoop, calls=%fused_computation.3 | loop fusion | flops 6291456 | bytes 8454144 | tf_op jit(solution)/shard_map/convert_element_type | solution.py:237
  126.9 12.6 %all-gather.5.cloned.1.call-done = bf16[32,4,128,128]{3,2,1,0:T(8,128)(2,1)} async-done(((bf16[1,4,128,128]{3,2,1,0:T(8,128)(2,1)}), bf16[32,4,128,128]{3,2,1,0:T(8,128)(2,1)}) %all-gather.5.cloned.1.call-update) | async-done | bytes 4194320 | tf_op jit(solution)/shard_map/all_gather | solution.py:199
  139.5 2.2 copy-done.3
  141.7 21.0 %attend.3 = (bf16[8,4,4,128,128]{4,3,2,1,0:T(8,128)(2,1)S(1)}, f32[4,8,512]{2,1,0:T(8,128)S(1)}, f32[4,8,512]{2,1,0:T(8,128)S(1)}) custom-call(s32[4]{0:T(128)S(1)} %get-tuple-element.42.live_ref, bf16[8,4,4,128,128]{4,3,2,1,0:T(8,128)(2,1)S(1)} %bitcast.64, bf16[8,512,1024]{2,1,0:T(8,128)(2,1)} %k_ref.3, bf16[8,512,1024]{2,1,0:T(8,128)(2,1)} %v_ref.3), custom_call_target="tpu_custom_call" | custom-call | flops 8589934592 | bytes 16777216 | tf_op jit(solution)/shard_map/attend/pallas_call | solution.py:72
  162.7 2.0 copy-done.2
  165.3 0.7 pad_maximum_fusion.1.st_ref
  166.0 18.1 %peaks.3 = (f32[8,4,4,128]{3,2,1,0:T(4,128)}, f32[8,128]{1,0:T(8,128)}) custom-call(f32[8,4,8,128]{3,2,1,0:T(8,128)} %pad_maximum_fusion.1.st_ref), custom_call_target="tpu_custom_call" | custom-call | tf_op jit(solution)/shard_map/peaks/pallas_call | solution.py:163
  184.1 0.9 multiply_exponential_fusion
  185.0 5.9 %fusion = bf16[32,4,128,128]{3,2,1,0:T(8,128)(2,1)} fusion(bf16[8,4,4,128,128]{4,3,2,1,0:T(8,128)(2,1)} %copy-done.2, f32[32,4,128]{2,1,0:T(4,128)S(1)} %bitcast.80), kind=kLoop, calls=%fused_computation.1 | loop fusion | flops 6291456 | bytes 8454144 | tf_op jit(solution)/shard_map/convert_element_type | solution.py:237
  191.9 1.3 fusion.4
  194.7 94.9 %reduce-scatter.3.cloned.1.call-done = bf16[1,4,128,128]{3,2,1,0:T(8,128)(2,1)} async-done(((bf16[32,4,128,128]{3,2,1,0:T(8,128)(2,1)}), bf16[1,4,128,128]{3,2,1,0:T(8,128)(2,1)}) %reduce-scatter.3.cloned.1.call-update) | async-done | bytes 131088 | tf_op jit(solution)/shard_map/reduce_scatter | solution.py:236
  289.6 0.9 convert.13
  290.6 149.2 %reduce-scatter.5.cloned.1.call-done = bf16[1,4,128,128]{3,2,1,0:T(8,128)(2,1)} async-done(((bf16[32,4,128,128]{3,2,1,0:T(8,128)(2,1)}), bf16[1,4,128,128]{3,2,1,0:T(8,128)(2,1)}) %reduce-scatter.5.cloned.1.call-update) | async-done | bytes 131088 | tf_op jit(solution)/shard_map/reduce_scatter | solution.py:236
  439.8 0.9 convert.15
  441.3 0.8 convert_element_type.60
  (65 shorter events, 6.0 us)
Async XLA Ops:
  6.5 184.4 %copy-start = (bf16[1024,1024]{1,0:T(8,128)(2,1)S(1)}, bf16[1024,1024]{1,0:T(8,128)(2,1)}, u32[]{:S(2)}) copy-start(bf16[1024,1024]{1,0:T(8,128)(2,1)} %param.11) | copy-start | bytes 6291460
  6.5 68.2 %all-gather.3.cloned.1.call-start = ((), (), s32[]{:S(2)}) async-start(), calls=%async_computation.2 | async-start | bytes 4325376 | tf_op jit(solution)/shard_map/all_gather | solution.py:199
  8.4 131.1 %all-gather.5.cloned.1.call-start = ((), (), s32[]{:S(2)}) async-start(), calls=%async_computation.4 | async-start | bytes 4325376 | tf_op jit(solution)/shard_map/all_gather | solution.py:199
  9.2 280.4 %reduce-scatter.3.cloned.1.call-start = ((), (), s32[]{:S(2)}) async-start(), calls=%async_computation.3 | async-start | bytes 4325376 | tf_op jit(solution)/shard_map/reduce_scatter | solution.py:236
  74.7 2.2 copy-start.4
  97.9 2.0 copy-start.1
  126.7 313.1 %reduce-scatter.5.cloned.1.call-start = ((), (), s32[]{:S(2)}) async-start(), calls=%async_computation.5 | async-start | bytes 4325376 | tf_op jit(solution)/shard_map/reduce_scatter | solution.py:236
  139.5 2.2 copy-start.3
  162.7 2.0 copy-start.2
  190.9 0.7 copy-start.5
  190.9 3.0 copy-start.6
  190.9 3.4 copy-start.7
Sparse Core Ops, SparseCore 0:
  10.3 64.3 all-gather.2
  77.7 61.7 all-gather.4
  141.8 147.7 reduce-scatter.2
  291.8 147.9 reduce-scatter.4

commit v2 on v1

--- a/solution.py
+++ b/solution.py
@@ -196,7 +196,7 @@
     some = users // CHUNKS
 
     gathered = [
-        lax.all_gather(q_local[i * some : (i + 1) * some], ("row", "col"), axis=0)
+        lax.all_gather(lax.all_gather(q_local[i * some : (i + 1) * some], "col"), "row")
         for i in range(CHUNKS)
     ]
 
@@ -214,12 +214,12 @@
     q_heads = q_local.astype(jnp.float32).reshape(users, kv_part, GROUP, beam_part, HD)
     own_score = jnp.sum(q_heads * own_keys, axis=-1) * (HD ** (-0.5) * LOG2E)
 
-    outs = []
+    sent, owns = [], []
     for i in range(CHUNKS):
         span = slice(i * some, (i + 1) * some)
         numer, m, l = attend(
             live[span],
-            gathered[i].reshape(rows, cols, some, piece, HD),
+            gathered[i],
             key_cache,
             value_cache,
             i * some,
@@ -231,20 +231,22 @@
 
         m = by_device(m)
         peak_all, own = peaks(jnp.concatenate([m, by_device(l)], axis=2))
-        factor = jnp.exp2(m - peak_all).reshape(rows * cols, some, piece)
-        weighted = numer.reshape(rows * cols, some, piece, HD).astype(jnp.float32) * factor[..., None]
-        numer = lax.psum_scatter(
-            weighted.astype(jnp.bfloat16), ("row", "col"), scatter_dimension=0, tiled=False
+        factor = jnp.exp2(m - peak_all).reshape(rows, cols, some, piece)
+        weighted = numer.astype(jnp.float32) * factor[..., None]
+        sent.append(
+            lax.psum_scatter(weighted.astype(jnp.bfloat16), "row", scatter_dimension=0, tiled=False)
         )
-        numer = numer.astype(jnp.float32).reshape(some, kv_part, GROUP, beam_part, HD)
-        peak, total = own.reshape(2, some, kv_part, GROUP, beam_part)
-        e = own_score[span]
-        top = jnp.maximum(peak, e)
-        carried = jnp.exp2(peak - top)
-        fresh = jnp.exp2(e - top)
-        numer = numer * carried[..., None] + fresh[..., None] * own_values[span]
-        outs.append(numer / (total * carried + fresh)[..., None])
-    result = jnp.concatenate(outs).reshape(users, heads_part, beam_part, HD)
+        owns.append(own.reshape(2, some, kv_part, GROUP, beam_part))
+
+    numer = lax.psum_scatter(jnp.concatenate(sent, axis=1), "col", scatter_dimension=0, tiled=False)
+    numer = numer.astype(jnp.float32).reshape(users, kv_part, GROUP, beam_part, HD)
+    peak, total = jnp.concatenate(owns, axis=1)
+    top = jnp.maximum(peak, own_score)
+    carried = jnp.exp2(peak - top)
+    fresh = jnp.exp2(own_score - top)
+    numer = numer * carried[..., None] + fresh[..., None] * own_values
+    result = numer / (total * carried + fresh)[..., None]
+    result = result.reshape(users, heads_part, beam_part, HD)
     return result.transpose(0, 2, 1, 3).reshape(users, beam_part, width_part).astype(jnp.bfloat16)
 
 

time: 449 us -> 262 us (0.58)
  waiting for transfers between devices: 322 us -> 99.3 us
  blocking collectives: 0 us -> 35.1 us
    reduce_scatter x2 -> x3, waiting for transfers between devices: 244 us -> 77.9 us  [the longest x2 52.9 us: body(): lax.psum_scatter(weighted.astype(jnp.bfloat16), 'row', scatter_dimension=...]
    all_gather x2, waiting for transfers between devices: 77.3 us -> 21.4 us  [body(): lax.all_gather(lax.all_gather(q_local[i * some:(i + 1) * some], 'col'), '...]
    all_gather x0 -> x2, blocking collectives: none -> 35.1 us  [body(): lax.all_gather(q_local[i * some:(i + 1) * some], 'col')]
    unnamed x17 -> x19, local copies, waits for them, and re-layouts: 10.1 us -> 9.48 us
  transfers between devices with their start and end apart: 4 -> 5, of which waited for: 4 -> 3; matrix products, arithmetic and copies ran while one was open for 5% -> 7% of each run, Pallas kernels for 18% -> 31%
where the time goes in v2:
time: 262 us; the launch traced here: 261 us
  waiting for transfers between devices  99.3 us (38%)
  Pallas kernels  80.5 us (31%)
  blocking collectives  35.1 us (13%)
  other arithmetic  19.5 us (7%)
  between operations  13.5 us (5%)
  local copies, waits for them, and re-layouts  11.4 us (4%)
    reduce_scatter x2, waiting for transfers between devices, body(): lax.psum_scatter(weighted.astype(jnp.bfloat16), 'row', scatter_dimension=...  52.9 us
    pallas_call x2, Pallas kernels, attend(): pl.pallas_call(attend_kernel, grid_spec=pltpu.PrefetchScalarGridSpec(num_...  42 us
    pallas_call x2, Pallas kernels, peaks(): pl.pallas_call(peaks_kernel, out_shape=[jax.ShapeDtypeStruct((rows, cols,...  38.5 us
    all_gather x2, blocking collectives, body(): lax.all_gather(q_local[i * some:(i + 1) * some], 'col')  35.1 us
    reduce_scatter x1, waiting for transfers between devices, body(): lax.psum_scatter(jnp.concatenate(sent, axis=1), 'col', scatter_dimension=...  24.9 us
    all_gather x2, waiting for transfers between devices, body(): lax.all_gather(lax.all_gather(q_local[i * some:(i + 1) * some], 'col'), '...  21.4 us
    convert_element_type x2, other arithmetic, body(): weighted.astype(jnp.bfloat16)  11.7 us
    unnamed x19, local copies, waits for them, and re-layouts  9.48 us
  transfers between devices with their start and end apart: 5, of which 3 were waited for; matrix products, arithmetic and copies ran while one was open for 7% of the time, Pallas kernels for 31%

profile of v2, /device:TPU:0, one launch (start us, length us, event | category | flops | bytes accessed | tf_op | source)
XLA Modules:
  0.0 261.2 jit_solution(1729439665493400822)
XLA Ops:
  6.5 1.2 copy.60
  7.8 18.0 %all_gather.29 = bf16[4,4,128,128]{3,2,1,0:T(8,128)(2,1)} all-gather(bf16[1,4,128,128]{3,2,1,0:T(8,128)(2,1)S(1)} %bitcast.58), channel_id=1, replica_groups=mesh['row'=8,'col'=4] {'col'}, dimensions={0}, use_global_device_ids=true | all-gather | bytes 655360 | tf_op jit(solution)/shard_map/all_gather | solution.py:199
  25.9 17.1 %all_gather.25 = bf16[4,4,128,128]{3,2,1,0:T(8,128)(2,1)} all-gather(bf16[1,4,128,128]{3,2,1,0:T(8,128)(2,1)S(1)} %bitcast.59), channel_id=1, replica_groups=mesh['row'=8,'col'=4] {'col'}, dimensions={0}, use_global_device_ids=true | all-gather | bytes 655360 | tf_op jit(solution)/shard_map/all_gather | solution.py:199
  43.2 21.3 %all-gather.7.cloned.1.call-done = bf16[32,4,128,128]{3,2,1,0:T(8,128)(2,1)} async-done(((bf16[4,4,128,128]{3,2,1,0:T(8,128)(2,1)}), bf16[32,4,128,128]{3,2,1,0:T(8,128)(2,1)}) %all-gather.7.cloned.1.call-update) | async-done | bytes 4194320 | tf_op jit(solution)/shard_map/all_gather | solution.py:199
  64.5 2.2 copy-done.4
  66.7 21.0 %attend.3 = (bf16[8,4,4,128,128]{4,3,2,1,0:T(8,128)(2,1)S(1)}, f32[4,8,512]{2,1,0:T(8,128)S(1)}, f32[4,8,512]{2,1,0:T(8,128)S(1)}) custom-call(s32[4]{0:T(128)S(1)} %get-tuple-element.33.live_ref, bf16[8,4,4,128,128]{4,3,2,1,0:T(8,128)(2,1)S(1)} %bitcast.52, bf16[8,512,1024]{2,1,0:T(8,128)(2,1)} %k_ref.3, bf16[8,512,1024]{2,1,0:T(8,128)(2,1)} %v_ref.3), custom_call_target="tpu_custom_call" | custom-call | flops 8589934592 | bytes 16777216 | tf_op jit(solution)/shard_map/attend/pallas_call | solution.py:72
  87.7 2.0 copy-done.1
  90.3 0.7 pad_maximum_fusion.2.st_ref
  91.0 20.2 %peaks.3 = (f32[8,4,4,128]{3,2,1,0:T(4,128)}, f32[8,128]{1,0:T(8,128)}) custom-call(f32[8,4,8,128]{3,2,1,0:T(8,128)} %pad_maximum_fusion.2.st_ref), custom_call_target="tpu_custom_call" | custom-call | tf_op jit(solution)/shard_map/peaks/pallas_call | solution.py:163
  111.2 0.9 multiply_exponential_fusion
  112.1 5.8 %multiply_convert_fusion = bf16[8,4,4,128,128]{4,3,2,1,0:T(8,128)(2,1)} fusion(bf16[8,4,4,128,128]{4,3,2,1,0:T(8,128)(2,1)} %copy-done.1, f32[8,4,4,128]{3,2,1,0:T(4,128)S(1)} %multiply_exponential_fusion), kind=kLoop, calls=%fused_computation | loop fusion | flops 6291456 | bytes 8454144 | tf_op jit(solution)/shard_map/convert_element_type | solution.py:237
  118.2 2.2 copy-done.3
  120.4 21.0 %attend.2 = (bf16[8,4,4,128,128]{4,3,2,1,0:T(8,128)(2,1)S(1)}, f32[4,8,512]{2,1,0:T(8,128)S(1)}, f32[4,8,512]{2,1,0:T(8,128)S(1)}) custom-call(s32[4]{0:T(128)S(1)} %get-tuple-element.32.live_ref, bf16[8,4,4,128,128]{4,3,2,1,0:T(8,128)(2,1)S(1)} %bitcast.51, bf16[8,512,1024]{2,1,0:T(8,128)(2,1)} %k_ref.3, bf16[8,512,1024]{2,1,0:T(8,128)(2,1)} %v_ref.3), custom_call_target="tpu_custom_call" | custom-call | flops 8589934592 | bytes 16777216 | tf_op jit(solution)/shard_map/attend/pallas_call | solution.py:72
  141.4 2.0 copy-done.2
  144.0 0.7 pad_maximum_fusion.1.st_ref
  144.7 18.3 %peaks.2 = (f32[8,4,4,128]{3,2,1,0:T(4,128)}, f32[8,128]{1,0:T(8,128)}) custom-call(f32[8,4,8,128]{3,2,1,0:T(8,128)} %pad_maximum_fusion.1.st_ref), custom_call_target="tpu_custom_call" | custom-call | tf_op jit(solution)/shard_map/peaks/pallas_call | solution.py:163
  163.0 0.9 multiply_exponential_fusion.1
  163.8 5.9 %multiply_convert_fusion.1 = bf16[8,4,4,128,128]{4,3,2,1,0:T(8,128)(2,1)} fusion(bf16[8,4,4,128,128]{4,3,2,1,0:T(8,128)(2,1)} %copy-done.2, f32[8,4,4,128]{3,2,1,0:T(4,128)S(1)} %multiply_exponential_fusion.1), kind=kLoop, calls=%fused_computation.1 | loop fusion | flops 6291456 | bytes 8454144 | tf_op jit(solution)/shard_map/convert_element_type | solution.py:237
  169.9 52.9 %reduce-scatter.4.cloned.1.call-done = bf16[1,4,4,128,128]{4,3,2,1,0:T(8,128)(2,1)} async-done(((bf16[8,4,4,128,128]{4,3,2,1,0:T(8,128)(2,1)}), bf16[1,4,4,128,128]{4,3,2,1,0:T(8,128)(2,1)}) %reduce-scatter.4.cloned.1.call-update) | async-done | bytes 524304 | tf_op jit(solution)/shard_map/reduce_scatter | solution.py:237
  222.8 2.3 pad_maximum_fusion
  225.1 0.3 fusion.5
  225.5 1.3 fusion.3
  227.6 24.9 %reduce-scatter.8.cloned.1.call-done = bf16[1,8,128,128]{3,2,1,0:T(8,128)(2,1)} async-done(((bf16[4,8,128,128]{3,2,1,0:T(8,128)(2,1)}), bf16[1,8,128,128]{3,2,1,0:T(8,128)(2,1)}) %reduce-scatter.8.cloned.1.call-update) | async-done | bytes 262160 | tf_op jit(solution)/shard_map/reduce_scatter | solution.py:241
  252.6 2.1 copy_bitcast_fusion
  (57 shorter events, 2.7 us)
Async XLA Ops:
  6.5 218.6 %copy-start = (bf16[1024,1024]{1,0:T(8,128)(2,1)S(1)}, bf16[1024,1024]{1,0:T(8,128)(2,1)}, u32[]{:S(2)}) copy-start(bf16[1024,1024]{1,0:T(8,128)(2,1)} %param.10) | copy-start | bytes 6291460
  6.5 36.5 %copy-start.8 = (s32[8]{0:T(128)S(1)}, s32[8]{0:T(128)}, u32[]{:S(2)}) copy-start(s32[8]{0:T(128)} %param.12) | copy-start | bytes 100
  6.5 58.0 %all-gather.7.cloned.1.call-start = ((), (), s32[]{:S(2)}) async-start(), calls=%async_computation.7 | async-start | bytes 4718592 | tf_op jit(solution)/shard_map/all_gather | solution.py:199
  25.8 92.4 %all-gather.5.cloned.1.call-start = ((), (), s32[]{:S(2)}) async-start(), calls=%async_computation.6 | async-start | bytes 4718592 | tf_op jit(solution)/shard_map/all_gather | solution.py:199
  43.0 126.8 %reduce-scatter.6.cloned.1.call-start = ((), (), s32[]{:S(2)}) async-start(), calls=%async_computation.4 | async-start | bytes 4718592 | tf_op jit(solution)/shard_map/reduce_scatter | solution.py:237
  64.5 2.2 copy-start.4
  87.7 2.0 copy-start.1
  117.9 104.9 %reduce-scatter.4.cloned.1.call-start = ((), (), s32[]{:S(2)}) async-start(), calls=%async_computation.3 | async-start | bytes 4718592 | tf_op jit(solution)/shard_map/reduce_scatter | solution.py:237
  118.2 2.2 copy-start.3
  141.4 2.0 copy-start.2
  169.7 55.4 %copy-start.5 = (s32[8,16]{1,0:T(8,128)S(1)}, s32[8,16]{1,0:T(8,128)}, u32[]{:S(2)}) copy-start(s32[8,16]{1,0:T(8,128)} %param.13) | copy-start | bytes 1540
  169.8 57.5 %copy-start.6 = (f32[8,128]{1,0:T(8,128)S(1)}, f32[8,128]{1,0:T(8,128)}, u32[]{:S(2)}) copy-start(f32[8,128]{1,0:T(8,128)} %get-tuple-element.24) | copy-start | bytes 12292
  169.8 57.7 %copy-start.7 = (f32[8,128]{1,0:T(8,128)S(1)}, f32[8,128]{1,0:T(8,128)}, u32[]{:S(2)}) copy-start(f32[8,128]{1,0:T(8,128)} %get-tuple-element.23) | copy-start | bytes 12292
  169.8 82.8 %reduce-scatter.8.cloned.1.call-start = ((), (), s32[]{:S(2)}) async-start(), calls=%async_computation.5 | async-start | bytes 1310720 | tf_op jit(solution)/shard_map/reduce_scatter | solution.py:241
Sparse Core Ops, SparseCore 0:
  25.9 38.5 all-gather.6
  66.4 37.9 all-gather.4
  118.0 50.5 reduce-scatter.5
  171.8 50.9 reduce-scatter.3
  225.2 27.2 reduce-scatter.7
